TPU v7x, 32 devices: a whole 2x2x4 slice. The times are simulated.
32 devices in a mesh: dp: 8 (over y, x, core), tensor: 4 (over z).
Axes of the slice: x: 2, y: 2, z: 4, core: 2. Of those that a mesh axis runs over, the one named last changes fastest.
Arguments:
- hidden_in: bfloat16 [8192, 2048], P(('dp', 'tensor')), may hold values from -6 to 6
- qkv_weight: bfloat16 [3, 2048, 2048], P(None, 'dp', 'tensor'), may hold values from -0.125 to 0.125
- head_bias: float32 [3, 2048], P(None, 'tensor'), may hold values from -3 to 3
- dense_weight: bfloat16 [2048, 2048], P('tensor', 'dp'), may hold values from -1 to 1
- dense_bias: float32 [2048], replicated, may hold values from -3 to 3
- fc1_weight: bfloat16 [2048, 8192], P('dp', 'tensor'), may hold values from -0.125 to 0.125
- fc1_bias: float32 [8192], P('tensor'), may hold values from -3 to 3
- fc2_weight: bfloat16 [8192, 2048], P('tensor', 'dp'), may hold values from -0.0625 to 0.0625
- fc2_bias: float32 [2048], replicated, may hold values from -3 to 3
- norm_gain: float32 [2048], replicated, may hold values from 0.5 to 1.5
- norm_bias: float32 [2048], replicated, may hold values from -2 to 2
- out_grad: bfloat16 [8192, 2048], P(('dp', 'tensor')), may hold values from -6 to 6
Outputs:
- hidden_out: bfloat16 [8192, 2048], P(('dp', 'tensor'))
- hidden_grad: bfloat16 [8192, 2048], P(('dp', 'tensor'))
- qkv_weight_grad: float32 [3, 2048, 2048], P(None, 'dp', 'tensor')
- head_bias_grad: float32 [3, 2048], P(None, 'tensor')
- dense_weight_grad: float32 [2048, 2048], P('tensor', 'dp')
- dense_bias_grad: float32 [2048], replicated
- fc1_weight_grad: float32 [2048, 8192], P('dp', 'tensor')
- fc1_bias_grad: float32 [8192], P('tensor')
- fc2_weight_grad: float32 [8192, 2048], P('tensor', 'dp')
- fc2_bias_grad: float32 [2048], replicated
- norm_gain_grad: float32 [2048], replicated
- norm_bias_grad: float32 [2048], replicated
All inputs are finite; a program needn't handle non-finite values.
Results may differ from a plain program's by a relative error of at most 0.0095.
Values may be sent and summed in bfloat16 or wider, within the bound.
A program may use at most 256 MiB of HBM per device.

v0:
```python
import math
import jax
import jax.numpy as jnp
from jax import lax
from jax.sharding import PartitionSpec as P

HD = 64
ROT = 32
SEQ_LEN = 1024


def dot_right(left, right):
    return lax.dot_general(
        left, right, (((1,), (1,)), ((), ())), preferred_element_type=jnp.float32
    )


def dot_left(left, right):
    return lax.dot_general(
        left, right, (((0,), (0,)), ((), ())), preferred_element_type=jnp.float32
    )


def gelu_tanh(values):
    return (
        0.5
        * values
        * (1.0 + jnp.tanh(0.7978845608028654 * (values + 0.044715 * values * values * values)))
    )


def rotate(values, sign):
    length = values.shape[0]
    half = ROT // 2
    freqs = 1.0 / 10000.0 ** (jnp.arange(half, dtype=jnp.float32) * 2.0 / ROT)
    positions = (jnp.arange(length) % SEQ_LEN).astype(jnp.float32)
    angles = positions[:, None] * freqs[None, :]
    cosine = jnp.cos(angles)[:, None, :]
    sine = sign * jnp.sin(angles)[:, None, :]
    first = values[..., :half]
    second = values[..., half:ROT]
    return jnp.concatenate(
        [first * cosine - second * sine, second * cosine + first * sine, values[..., ROT:]], axis=-1
    )


def masked_scores(queries, keys, start, finish, scale):
    scores = (
        jnp.einsum(
            "sqhd,skhd->shqk",
            queries[:, start:finish],
            keys[:, :finish],
            preferred_element_type=jnp.float32,
        )
        * scale
    )
    causal = jnp.arange(finish)[None, :] <= (jnp.arange(finish - start) + start)[:, None]
    return jnp.where(causal, scores, -1e30)


def attend(queries, keys, values):
    length = queries.shape[1]
    block = min(512, length)
    scale = 1.0 / math.sqrt(queries.shape[3])
    outputs = []
    logsums = []
    for block_index in range(length // block):
        start = block_index * block
        finish = start + block
        scores = masked_scores(queries, keys, start, finish, scale)
        largest = jnp.max(scores, axis=-1, keepdims=True)
        expos = jnp.exp(scores - largest)
        summed = jnp.sum(expos, axis=-1, keepdims=True)
        probs = (expos / summed).astype(jnp.bfloat16)
        outputs.append(
            jnp.einsum(
                "shqk,skhd->sqhd", probs, values[:, :finish], preferred_element_type=jnp.float32
            )
        )
        logsums.append((largest + jnp.log(summed))[..., 0])
    return (jnp.concatenate(outputs, axis=1), jnp.concatenate(logsums, axis=2))


def attend_back(queries, keys, values, grads_out, logsum):
    length = queries.shape[1]
    block = min(512, length)
    scale = 1.0 / math.sqrt(queries.shape[3])
    query_grads = []
    key_grad = jnp.zeros(keys.shape, jnp.float32)
    value_grad = jnp.zeros(values.shape, jnp.float32)
    for block_index in range(length // block):
        start = block_index * block
        finish = start + block
        scores = masked_scores(queries, keys, start, finish, scale)
        probs = jnp.exp(scores - logsum[:, :, start:finish, None])
        products = jnp.einsum(
            "sqhd,skhd->shqk",
            grads_out[:, start:finish],
            values[:, :finish],
            preferred_element_type=jnp.float32,
        )
        inner = jnp.sum(probs * products, axis=-1, keepdims=True)
        score_grad = (probs * (products - inner)).astype(jnp.bfloat16)
        query_grads.append(
            jnp.einsum(
                "shqk,skhd->sqhd", score_grad, keys[:, :finish], preferred_element_type=jnp.float32
            )
            * scale
        )
        key_grad = key_grad.at[:, :finish].add(
            jnp.einsum(
                "shqk,sqhd->skhd",
                score_grad,
                queries[:, start:finish],
                preferred_element_type=jnp.float32,
            )
            * scale
        )
        value_grad = value_grad.at[:, :finish].add(
            jnp.einsum(
                "shqk,sqhd->skhd",
                probs.astype(jnp.bfloat16),
                grads_out[:, start:finish],
                preferred_element_type=jnp.float32,
            )
        )
    return (jnp.concatenate(query_grads, axis=1), key_grad, value_grad)


def per_device(
    hidden_in,
    qkv_weight,
    head_bias,
    dense_weight,
    dense_bias,
    fc1_weight,
    fc1_bias,
    fc2_weight,
    fc2_bias,
    norm_gain,
    norm_bias,
    out_grad,
):
    qkv_full, dense_full, fc1_full, fc2_full = (
        lax.all_gather(qkv_weight, "dp", axis=1, tiled=True),
        lax.all_gather(dense_weight, "dp", axis=1, tiled=True),
        lax.all_gather(fc1_weight, "dp", axis=0, tiled=True),
        lax.all_gather(fc2_weight, "dp", axis=1, tiled=True),
    )
    inputs = hidden_in.astype(jnp.float32)
    centred = inputs - jnp.mean(inputs, axis=-1, keepdims=True)
    inverse_std = lax.rsqrt(jnp.mean(centred * centred, axis=-1, keepdims=True) + 1e-05)
    standard = centred * inverse_std
    normed = (standard * norm_gain + norm_bias).astype(jnp.bfloat16)
    normed_all = lax.all_gather(normed, "tensor", axis=0, tiled=True)
    rows = normed_all.shape[0]
    count = rows // SEQ_LEN
    width_local = qkv_full.shape[2]
    heads_local = width_local // HD

    def split_heads(values):
        return values.reshape(count, SEQ_LEN, heads_local, HD)

    projected = (
        jnp.einsum("td,cde->cte", normed_all, qkv_full, preferred_element_type=jnp.float32)
        + head_bias[:, None, :]
    )
    queries = rotate(projected[0].reshape(rows, heads_local, HD), 1.0).astype(jnp.bfloat16)
    keys = rotate(projected[1].reshape(rows, heads_local, HD), 1.0).astype(jnp.bfloat16)
    values = projected[2].astype(jnp.bfloat16).reshape(rows, heads_local, HD)
    mixed, logsum = attend(split_heads(queries), split_heads(keys), split_heads(values))
    mixed = mixed.reshape(rows, width_local).astype(jnp.bfloat16)
    hidden = jnp.dot(normed_all, fc1_full, preferred_element_type=jnp.float32) + fc1_bias
    active = gelu_tanh(hidden).astype(jnp.bfloat16)
    partial_value = jnp.dot(mixed, dense_full, preferred_element_type=jnp.float32) + jnp.dot(
        active, fc2_full, preferred_element_type=jnp.float32
    )
    summed = lax.psum_scatter(partial_value, "tensor", scatter_dimension=0, tiled=True)
    hidden_out = (inputs + summed + dense_bias + fc2_bias).astype(jnp.bfloat16)
    qkv_back, dense_back, fc1_back, fc2_back = (qkv_full, dense_full, fc1_full, fc2_full)
    grad_all = lax.all_gather(out_grad, "tensor", axis=0, tiled=True)
    feed_grad = dot_right(grad_all, fc2_back)
    unused, gelu_pull = jax.vjp(gelu_tanh, hidden)
    hidden_back = gelu_pull(feed_grad)[0].astype(jnp.bfloat16)
    fc2_grad = dot_left(active, grad_all)
    fc1_grad = dot_left(normed_all, hidden_back)
    fc1_bias_part = jnp.sum(hidden_back.astype(jnp.float32), axis=0)
    normed_back = dot_right(hidden_back, fc1_back)
    mixed_back = dot_right(grad_all, dense_back).astype(jnp.bfloat16)
    dense_grad = dot_left(mixed, grad_all)
    query_back, key_back, value_back = attend_back(
        split_heads(queries),
        split_heads(keys),
        split_heads(values),
        split_heads(mixed_back),
        logsum,
    )
    query_back = rotate(query_back.reshape(rows, heads_local, HD), -1.0).reshape(rows, width_local)
    key_back = rotate(key_back.reshape(rows, heads_local, HD), -1.0).reshape(rows, width_local)
    proj_back = jnp.stack([query_back, key_back, value_back.reshape(rows, width_local)]).astype(
        jnp.bfloat16
    )
    qkv_grad = jnp.einsum("td,cte->cde", normed_all, proj_back, preferred_element_type=jnp.float32)
    head_bias_part = jnp.sum(proj_back.astype(jnp.float32), axis=1)
    normed_back = normed_back + jnp.einsum(
        "cte,cde->td", proj_back, qkv_back, preferred_element_type=jnp.float32
    )
    own_back = lax.psum_scatter(normed_back, "tensor", scatter_dimension=0, tiled=True)
    scaled = own_back * norm_gain
    hidden_grad = out_grad.astype(jnp.float32) + inverse_std * (
        scaled
        - jnp.mean(scaled, axis=-1, keepdims=True)
        - standard * jnp.mean(scaled * standard, axis=-1, keepdims=True)
    )
    gain_part = jnp.sum(own_back * standard, axis=0)
    shift_part = jnp.sum(own_back, axis=0)
    output_part = jnp.sum(out_grad.astype(jnp.float32), axis=0)
    gain_grad, shift_grad, output_bias_grad = lax.psum(
        (gain_part, shift_part, output_part), ("dp", "tensor")
    )
    head_bias_grad, fc1_bias_grad = lax.psum((head_bias_part, fc1_bias_part), "dp")
    qkv_grad, dense_grad, fc1_grad, fc2_grad = (
        lax.psum_scatter(qkv_grad, "dp", scatter_dimension=1, tiled=True),
        lax.psum_scatter(dense_grad, "dp", scatter_dimension=1, tiled=True),
        lax.psum_scatter(fc1_grad, "dp", scatter_dimension=0, tiled=True),
        lax.psum_scatter(fc2_grad, "dp", scatter_dimension=1, tiled=True),
    )
    return (
        hidden_out,
        hidden_grad.astype(jnp.bfloat16),
        qkv_grad,
        head_bias_grad,
        dense_grad,
        output_bias_grad,
        fc1_grad,
        fc1_bias_grad,
        fc2_grad,
        output_bias_grad,
        gain_grad,
        shift_grad,
    )


def solution(mesh):
    placed = (
        P(("dp", "tensor"), None),
        P(None, "dp", "tensor"),
        P(None, "tensor"),
        P("tensor", "dp"),
        P(),
        P("dp", "tensor"),
        P("tensor"),
        P("tensor", "dp"),
        P(),
        P(),
        P(),
        P(("dp", "tensor"), None),
    )
    return jax.shard_map(
        per_device,
        mesh=mesh,
        in_specs=placed,
        out_specs=(
            P(("dp", "tensor"), None),
            P(("dp", "tensor"), None),
            P(None, "dp", "tensor"),
            P(None, "tensor"),
            P("tensor", "dp"),
            P(),
            P("dp", "tensor"),
            P("tensor"),
            P("tensor", "dp"),
            P(),
            P(),
            P(),
        ),
        check_vma=False,
    )
```

profile of v0, /device:TPU:0, one launch (start us, length us, event | category | flops | bytes accessed | tf_op | source)
XLA Modules:
  0.0 1059.4 jit_solution(7889824522170710664)
XLA Ops:
  10.2 1.6 fusion.35
  12.4 2.7 fusion.30
  19.7 21.1 %all-gather.11.cloned.1.call-done = bf16[512,2048]{1,0:T(8,128)(2,1)} async-done(((bf16[512,256]{1,0:T(8,128)(2,1)}), bf16[512,2048]{1,0:T(8,128)(2,1)}) %all-gather.11.cloned.1.call-update) | async-done | bytes 2097168 | tf_op jit(solution)/shard_map/all_gather | solution.py:146
  40.7 82.3 %all-gather.17.cloned.1.call-done = bf16[1024,2048]{1,0:T(8,128)(2,1)} async-done(((bf16[256,2048]{1,0:T(8,128)(2,1)}), bf16[1024,2048]{1,0:T(8,128)(2,1)}) %all-gather.17.cloned.1.call-update) | async-done | bytes 4194320 | tf_op jit(solution)/shard_map/all_gather | solution.py:181
  123.1 6.2 convolution_convert_fusion
  129.3 75.2 %all-gather.7.cloned.1.call-done = bf16[1024,2048]{1,0:T(8,128)(2,1)} async-done(((bf16[256,2048]{1,0:T(8,128)(2,1)}), bf16[1024,2048]{1,0:T(8,128)(2,1)}) %all-gather.7.cloned.1.call-update) | async-done | bytes 4194320 | tf_op jit(solution)/shard_map/all_gather | solution.py:155
  204.5 47.4 %all-gather.9.cloned.1.call-done = bf16[3,2048,512]{1,2,0:T(8,128)(2,1)} async-done(((bf16[3,256,512]{1,2,0:T(8,128)(2,1)}), bf16[3,2048,512]{1,2,0:T(8,128)(2,1)}) %all-gather.9.cloned.1.call-update) | async-done | bytes 6291472 | tf_op jit(solution)/shard_map/all_gather | solution.py:145
  251.9 10.6 %add_bitcast_fusion = f32[3,1024,512]{1,2,0:T(8,128)S(1)} fusion(f32[3,512]{1,0:T(4,128)S(1)} %copy-done.40, bf16[3,2048,512]{1,2,0:T(8,128)(2,1)} %all-gather.9.cloned.1.call-done, bf16[1024,2048]{1,0:T(8,128)(2,1)} %all-gather.7.cloned.1.call-done), kind=kOutput, calls=%fused_computation.33 | convolution fusion | flops 6444023808 | bytes 16783360 | tf_op jit(solution)/shard_map/td,cde->cte/dot_general | solution.py:165
  264.7 1.6 fusion.72
  267.5 2.1 copy-done.1
  269.6 3.2 fusion.73
  272.8 3.8 fusion
  276.6 5.5 copy-done.2
  284.2 4.0 fusion.40
  288.2 2.3 copy.31
  290.5 7.6 multiply_reduce_fusion.1
  298.0 7.4 multiply_convert_fusion.1
  305.5 2.1 copy-done.3
  307.6 1.8 fusion.48
  309.4 9.9 multiply_reduce_fusion
  319.3 10.4 multiply_convert_fusion
  329.7 6.3 fusion.49
  338.9 1.6 fusion.41
  342.5 2.3 copy.29
  344.8 2.3 copy.30
  347.1 12.4 %convolution_bitcast_fusion = f32[3,2048,512]{1,2,0:T(8,128)} fusion(bf16[1024,2048]{1,0:T(8,128)(2,1)} %all-gather.7.cloned.1.call-done, bf16[1,1024,512]{2,1,0:T(8,128)(2,1)S(1)} %copy-done.7, bf16[1,1024,512]{2,1,0:T(8,128)(2,1)} %copy.30, bf16[1,1024,512]{2,1,0:T(8,128)(2,1)} %copy.29), kind=kOutput, calls=%fused_computation.34 | convolution fusion | flops 6445596672 | bytes 19922944 | tf_op jit(solution)/shard_map/td,cte->cde/dot_general | solution.py:203
  359.6 14.6 %fusion.74 = f32[1024,2048]{1,0:T(8,128)} fusion(bf16[1024,2048]{1,0:T(8,128)(2,1)} %all-gather.7.cloned.1.call-done, bf16[2048,2048]{1,0:T(8,128)(2,1)} %all-gather.13.cloned.1.call-done), kind=kOutput, calls=%fused_computation.141 | convolution fusion | flops 8589934592 | bytes 20971520 | tf_op jit(solution)/shard_map/dot_general | solution.py:173
  374.2 22.7 %convert_reduce_fusion = (f32[2048]{0:T(1024)}, bf16[1024,2048]{1,0:T(8,128)(2,1)S(1)}) fusion(f32[1024,2048]{1,0:T(8,128)} %fusion.74, f32[2048]{0:T(1024)S(1)} %copy-done.41, bf16[1024,2048]{1,0:T(8,128)(2,1)} %all-gather.17.cloned.1.call-done, bf16[2048,2048]{1,0:T(8,128)(2,1)} %all-gather.15.cloned.1.call-done), kind=kOutput, calls=%fused_computation.20 | convolution fusion | flops 8646555648 | bytes 25182208 | tf_op jit(solution)/shard_map/dot_general | solution.py:13
  396.8 11.7 %fusion.75 = f32[1024,2048]{1,0:T(8,128)} fusion(bf16[1024,2048]{1,0:T(8,128)(2,1)S(1)} %get-tuple-element.98, bf16[2048,2048]{1,0:T(8,128)(2,1)S(1)} %copy-done.39), kind=kOutput, calls=%fused_computation.142 | convolution fusion | flops 8589934592 | bytes 20971520 | tf_op jit(solution)/shard_map/dot_general | solution.py:13
  408.5 13.2 %bitcast_add_fusion = f32[1024,2048]{1,0:T(8,128)} fusion(f32[1024,2048]{1,0:T(8,128)} %fusion.75, bf16[3,2048,512]{1,2,0:T(8,128)(2,1)} %all-gather.9.cloned.1.call-done, bf16[1,1024,512]{2,1,0:T(8,128)(2,1)S(1)} %copy-done.7, bf16[1,1024,512]{2,1,0:T(8,128)(2,1)S(1)} %copy-done.9, bf16[1,1024,512]{2,1,0:T(8,128)(2,1)S(1)} %copy-done.8), kind=kOutput, calls=%fused_computation.19 | convolution fusion | flops 6447693824 | bytes 26214400 | tf_op jit(solution)/shard_map/cte,cde->td/dot_general | solution.py:205
  422.4 5.0 fusion.53
  427.4 8.0 fusion.52
  435.6 12.2 %fusion.69 = f32[1024,2048]{1,0:T(8,128)S(1)} fusion(bf16[2048,2048]{1,0:T(8,128)(2,1)S(1)} %bitcast.159, f32[1024,2048]{1,0:T(8,128)} %fusion.74, f32[2048]{0:T(1024)S(1)} %copy-done.41), kind=kOutput, calls=%fused_computation.136 | convolution fusion | flops 8610906112 | bytes 25174016 | tf_op jit(solution)/shard_map/dot_general | solution.py:175
  447.8 5.7 convolution_add_fusion
  453.6 6.5 fusion.76
  460.2 17.5 %fusion.68 = f32[2048,2048]{1,0:T(8,128)} fusion(bf16[1024,2048]{1,0:T(8,128)(2,1)} %all-gather.17.cloned.1.call-done, f32[1024,2048]{1,0:T(8,128)} %fusion.74, f32[2048]{0:T(1024)S(1)} %copy-done.41), kind=kOutput, calls=%fused_computation.135 | convolution fusion | flops 8610906112 | bytes 29368320 | tf_op jit(solution)/shard_map/dot_general | solution.py:19
  477.7 15.5 %fusion.77 = f32[2048,2048]{1,0:T(8,128)} fusion(bf16[1024,2048]{1,0:T(8,128)(2,1)} %all-gather.7.cloned.1.call-done, bf16[1024,2048]{1,0:T(8,128)(2,1)} %copy-done.42), kind=kOutput, calls=%fused_computation.144 | convolution fusion | flops 8589934592 | bytes 25165824 | tf_op jit(solution)/shard_map/dot_general | solution.py:19
  493.3 2.1 convert_reduce_fusion.1
  495.4 24.6 %all-reduce.3 = (f32[3,512]{1,0:T(4,128)}, f32[2048]{0:T(1024)}) all-reduce(f32[3,512]{1,0:T(4,128)S(1)} %convert_reduce_fusion.1, f32[2048]{0:T(1024)S(1)} %copy-done.35), channel_id=1, replica_groups=mesh['dp'=8,'tensor'=4] {'dp'}, use_global_device_ids=true, to_apply=%region_14.15 | all-reduce | flops 3584 | bytes 28672 | tf_op jit(solution)/shard_map/psum | solution.py:221
  520.0 3.0 copy.34
  523.0 85.0 %reduce-scatter.9.cloned.1.call-done = f32[256,2048]{1,0:T(8,128)} async-done(((f32[1024,2048]{1,0:T(8,128)}), f32[256,2048]{1,0:T(8,128)}) %reduce-scatter.9.cloned.1.call-update) | async-done | bytes 2097168 | tf_op jit(solution)/shard_map/reduce_scatter | solution.py:208
  608.1 2.6 fusion.34
  610.7 145.0 %reduce-scatter.7.cloned.1.call-done = f32[256,2048]{1,0:T(8,128)} async-done(((f32[1024,2048]{1,0:T(8,128)}), f32[256,2048]{1,0:T(8,128)}) %reduce-scatter.7.cloned.1.call-update) | async-done | bytes 2097168 | tf_op jit(solution)/shard_map/reduce_scatter | solution.py:178
  755.7 5.1 convert_reduce_fusion.3
  760.8 41.3 %all-reduce.2 = (f32[2048]{0:T(1024)S(1)}, f32[2048]{0:T(1024)}, f32[2048]{0:T(1024)}) all-reduce(f32[2048]{0:T(1024)S(1)} %get-tuple-element.109, f32[2048]{0:T(1024)S(1)} %get-tuple-element.88, f32[2048]{0:T(1024)S(1)} %get-tuple-element.91), channel_id=1, replica_groups=mesh['dp'=8,'tensor'=4] {'dp','tensor'}, use_global_device_ids=true, to_apply=%region_17.18 | all-reduce | flops 6144 | bytes 49152 | tf_op jit(solution)/shard_map/psum | solution.py:218
  802.1 9.2 reduce-scatter.13.cloned.1.call-done
  811.3 120.2 %reduce-scatter.17.cloned.1.call-done = f32[2048,256]{1,0:T(8,128)} async-done(((f32[2048,2048]{1,0:T(8,128)}), f32[2048,256]{1,0:T(8,128)}) %reduce-scatter.17.cloned.1.call-update) | async-done | bytes 2097168 | tf_op jit(solution)/shard_map/reduce_scatter | solution.py:226
  931.5 120.2 %reduce-scatter.15.cloned.1.call-done = f32[256,2048]{1,0:T(8,128)} async-done(((f32[2048,2048]{1,0:T(8,128)}), f32[256,2048]{1,0:T(8,128)}) %reduce-scatter.15.cloned.1.call-update) | async-done | bytes 2097168 | tf_op jit(solution)/shard_map/reduce_scatter | solution.py:225
  (160 shorter events, 20.0 us)
Async XLA Ops:
  7.2 8.0 copy-start.16
  7.2 33.5 %all-gather.11.cloned.1.call-start = ((), (), s32[]{:S(2)}) async-start(), calls=%async_computation.8 | async-start | bytes 2359296 | tf_op jit(solution)/shard_map/all_gather | solution.py:146
  7.9 115.1 %all-gather.17.cloned.1.call-start = ((), (), s32[]{:S(2)}) async-start(), calls=%async_computation.12 | async-start | bytes 5242880 | tf_op jit(solution)/shard_map/all_gather | solution.py:181
  8.7 195.8 %all-gather.7.cloned.1.call-start = ((), (), s32[]{:S(2)}) async-start(), calls=%async_computation.6 | async-start | bytes 5242880 | tf_op jit(solution)/shard_map/all_gather | solution.py:155
  15.1 236.8 %all-gather.9.cloned.1.call-start = ((), (), s32[]{:S(2)}) async-start(), calls=%async_computation.7 | async-start | bytes 7077888 | tf_op jit(solution)/shard_map/all_gather | solution.py:145
  16.3 343.2 %all-gather.13.cloned.1.call-start = ((), (), s32[]{:S(2)}) async-start(), calls=%async_computation.9 | async-start | bytes 9437184 | tf_op jit(solution)/shard_map/all_gather | solution.py:147
  16.9 357.2 %all-gather.15.cloned.1.call-start = ((), (), s32[]{:S(2)}) async-start(), calls=%async_computation.10 | async-start | bytes 9437184 | tf_op jit(solution)/shard_map/all_gather | solution.py:148
  17.5 502.5 %reduce-scatter.11.cloned.1.call-start = ((), (), s32[]{:S(2)}) async-start(), calls=%async_computation.14 | async-start | bytes 14155776 | tf_op jit(solution)/shard_map/reduce_scatter | solution.py:223
  19.7 243.7 %copy-start.17 = (f32[1024,16]{0,1:T(8,128)}, f32[1024,16]{0,1:T(8,128)S(1)}, u32[]{:S(2)}) copy-start(f32[1024,16]{0,1:T(8,128)S(1)} %get-tuple-element.118) | copy-start | bytes 196612
  19.7 232.2 %copy-start.40 = (f32[3,512]{1,0:T(4,128)S(1)}, f32[3,512]{1,0:T(4,128)}, u32[]{:S(2)}) copy-start(f32[3,512]{1,0:T(4,128)} %param.26) | copy-start | bytes 18436
  263.3 6.3 copy-start.13
  266.3 6.5 copy-start.23
  269.6 20.8 %copy-start.21 = (f32[8,512]{1,0:T(8,128)}, f32[8,512]{1,0:T(8,128)S(1)}, u32[]{:S(2)}) copy-start(f32[8,512]{1,0:T(8,128)S(1)} %log_add_fusion.1) | copy-start | bytes 49156
  272.8 11.4 %copy-start = (f32[8,512,1024]{2,1,0:T(8,128)}, f32[8,512,1024]{2,1,0:T(8,128)S(1)}, u32[]{:S(2)}) copy-start(f32[8,512,1024]{2,1,0:T(8,128)S(1)} %get-tuple-element.122) | copy-start | bytes 50331652
  272.8 9.4 copy-start.2
  272.8 10.0 copy-start.6
  276.6 11.6 %copy-start.29 = (f32[8,512]{1,0:T(8,128)}, f32[8,512]{1,0:T(8,128)S(1)}, u32[]{:S(2)}) copy-start(f32[8,512]{1,0:T(8,128)S(1)} %fusion) | copy-start | bytes 49156
  290.4 18.9 %slice-start = ((s8[16777216]{0:T(1024)(128)(4,1)}), s8[4194304]{0:T(1024)(128)(4,1)S(1)}, s32[]{:S(2)}) async-start(s8[16777216]{0:T(1024)(128)(4,1)} %bitcast.132), calls=%async_computation.18 | async-start | bytes 8388608
  290.4 19.0 %slice-start.1 = ((s8[16777216]{0:T(1024)(128)(4,1)}), s8[4194304]{0:T(1024)(128)(4,1)S(1)}, s32[]{:S(2)}) async-start(s8[16777216]{0:T(1024)(128)(4,1)} %bitcast.132), calls=%async_computation.19 | async-start | bytes 8388608
  298.0 9.6 copy-start.15
  298.0 11.4 %slice-start.2 = ((s8[16777216]{0:T(1024)(128)(4,1)}), s8[4194304]{0:T(1024)(128)(4,1)S(1)}, s32[]{:S(2)}) async-start(s8[16777216]{0:T(1024)(128)(4,1)} %bitcast.132), calls=%async_computation.20 | async-start | bytes 8388608
  298.0 11.4 %slice-start.3 = ((s8[16777216]{0:T(1024)(128)(4,1)}), s8[4194304]{0:T(1024)(128)(4,1)S(1)}, s32[]{:S(2)}) async-start(s8[16777216]{0:T(1024)(128)(4,1)} %bitcast.132), calls=%async_computation.21 | async-start | bytes 8388608
  329.6 6.4 copy-start.10
  329.6 6.6 copy-start.4
  329.6 8.0 slice-start.4
  340.6 6.5 copy-start.7
  359.5 14.7 %copy-start.41 = (f32[2048]{0:T(1024)S(1)}, f32[2048]{0:T(1024)}, u32[]{:S(2)}) copy-start(f32[2048]{0:T(1024)} %param.30) | copy-start | bytes 24580
  359.5 248.5 %reduce-scatter.9.cloned.1.call-start = ((), (), s32[]{:S(2)}) async-start(), calls=%async_computation.13 | async-start | bytes 10485760 | tf_op jit(solution)/shard_map/reduce_scatter | solution.py:208
  374.2 22.7 %copy-start.39 = (bf16[2048,2048]{1,0:T(8,128)(2,1)S(1)}, bf16[2048,2048]{1,0:T(8,128)(2,1)}, u32[]{:S(2)}) copy-start(bf16[2048,2048]{1,0:T(8,128)(2,1)} %all-gather.13.cloned.1.call-done) | copy-start | bytes 25165828
  396.8 11.7 %copy-start.42 = (bf16[1024,2048]{1,0:T(8,128)(2,1)}, bf16[1024,2048]{1,0:T(8,128)(2,1)S(1)}, u32[]{:S(2)}) copy-start(bf16[1024,2048]{1,0:T(8,128)(2,1)S(1)} %get-tuple-element.98) | copy-start | bytes 12582916
  396.8 11.7 %copy-start.8 = (bf16[1,1024,512]{2,1,0:T(8,128)(2,1)S(1)}, bf16[1,1024,512]{2,1,0:T(8,128)(2,1)}, u32[]{:S(2)}) copy-start(bf16[1,1024,512]{2,1,0:T(8,128)(2,1)} %copy.29) | copy-start | bytes 3145732
  396.8 11.7 %copy-start.9 = (bf16[1,1024,512]{2,1,0:T(8,128)(2,1)S(1)}, bf16[1,1024,512]{2,1,0:T(8,128)(2,1)}, u32[]{:S(2)}) copy-start(bf16[1,1024,512]{2,1,0:T(8,128)(2,1)} %copy.30) | copy-start | bytes 3145732
  421.7 5.7 copy-start.28
  421.7 333.9 %reduce-scatter.7.cloned.1.call-start = ((), (), s32[]{:S(2)}) async-start(), calls=%async_computation.11 | async-start | bytes 10485760 | tf_op jit(solution)/shard_map/reduce_scatter | solution.py:178
  422.4 13.2 %slice-start.6 = ((s8[8388608]{0:T(1024)(128)(4,1)}), s8[4194304]{0:T(1024)(128)(4,1)S(1)}, s32[]{:S(2)}) async-start(s8[8388608]{0:T(1024)(128)(4,1)} %bitcast.158), calls=%async_computation.24 | async-start | bytes 8388608
  427.4 8.1 slice-start.7
  435.6 12.2 %copy-start.12 = (bf16[512,2048]{1,0:T(8,128)(2,1)S(1)}, bf16[512,2048]{1,0:T(8,128)(2,1)}, u32[]{:S(2)}) copy-start(bf16[512,2048]{1,0:T(8,128)(2,1)} %all-gather.11.cloned.1.call-done) | copy-start | bytes 6291460
  453.5 357.8 %reduce-scatter.13.cloned.1.call-start = ((), (), s32[]{:S(2)}) async-start(), calls=%async_computation.15 | async-start | bytes 4718592 | tf_op jit(solution)/shard_map/reduce_scatter | solution.py:224
  460.1 471.4 %reduce-scatter.17.cloned.1.call-start = ((), (), s32[]{:S(2)}) async-start(), calls=%async_computation.17 | async-start | bytes 18874368 | tf_op jit(solution)/shard_map/reduce_scatter | solution.py:226
  477.7 574.0 %reduce-scatter.15.cloned.1.call-start = ((), (), s32[]{:S(2)}) async-start(), calls=%async_computation.16 | async-start | bytes 18874368 | tf_op jit(solution)/shard_map/reduce_scatter | solution.py:225
  493.2 114.8 %copy-start.5 = (bf16[256,2048]{1,0:T(8,128)(2,1)S(1)}, bf16[256,2048]{1,0:T(8,128)(2,1)}, u32[]{:S(2)}) copy-start(bf16[256,2048]{1,0:T(8,128)(2,1)} %param.24) | copy-start | bytes 3145732
  493.2 114.8 %copy-start.22 = (f32[2048]{0:T(1024)S(1)}, f32[2048]{0:T(1024)}, u32[]{:S(2)}) copy-start(f32[2048]{0:T(1024)} %param.33) | copy-start | bytes 24580
  493.2 114.8 %copy-start.32 = (f32[256]{0:T(256)S(1)}, f32[256]{0:T(256)}, u32[]{:S(2)}) copy-start(f32[256]{0:T(256)} %copy-done.31) | copy-start | bytes 3076
  493.3 114.8 %copy-start.34 = (f32[256]{0:T(256)S(1)}, f32[256]{0:T(256)}, u32[]{:S(2)}) copy-start(f32[256]{0:T(256)} %copy-done.33) | copy-start | bytes 3076
  493.3 262.4 %copy-start.37 = (f32[2048]{0:T(1024)S(1)}, f32[2048]{0:T(1024)}, u32[]{:S(2)}) copy-start(f32[2048]{0:T(1024)} %param.32) | copy-start | bytes 24580
  493.3 262.4 %copy-start.38 = (f32[2048]{0:T(1024)S(1)}, f32[2048]{0:T(1024)}, u32[]{:S(2)}) copy-start(f32[2048]{0:T(1024)} %param.28) | copy-start | bytes 24580
  495.4 260.3 %copy-start.11 = (bf16[256,2048]{1,0:T(8,128)(2,1)S(1)}, bf16[256,2048]{1,0:T(8,128)(2,1)}, u32[]{:S(2)}) copy-start(bf16[256,2048]{1,0:T(8,128)(2,1)} %param.35) | copy-start | bytes 3145732
  802.1 250.2 %copy-start.36 = (f32[2048]{0:T(1024)}, f32[2048]{0:T(1024)S(1)}, u32[]{:S(2)}) copy-start(f32[2048]{0:T(1024)S(1)} %get-tuple-element.150) | copy-start | bytes 24580
  (15 other events, 32.8 us)
Sparse Core Ops, SparseCore 0:
  9.9 30.8 all-gather.10
  42.3 80.7 all-gather.16
  125.2 79.2 all-gather.6
  206.8 45.0 all-gather.8
  253.6 54.2 all-gather.12
  309.6 55.8 all-gather.14
  369.0 91.9 reduce-scatter.10
  463.4 144.6 reduce-scatter.8
  610.4 145.1 reduce-scatter.6
  759.4 51.8 reduce-scatter.12
  815.4 116.0 reduce-scatter.16
  935.5 116.1 reduce-scatter.14
where the time goes:
time: 1060 us
  waiting for transfers between devices  708 us (67%)
  matrix products  200 us (19%)
  blocking collectives  65.9 us (6%)
  other arithmetic  42.9 us (4%)
  local copies, waits for them, and re-layouts  26.5 us (2%)
  between operations  15.2 us (1%)
    reduce_scatter x1, waiting for transfers between devices, per_device(): lax.psum_scatter(partial_value, 'tensor', scatter_dimension=0, tiled=True)  145 us
    reduce_scatter x1, waiting for transfers between devices, per_device(): lax.psum_scatter(fc1_grad, 'dp', scatter_dimension=0, tiled=True)  120 us
    reduce_scatter x1, waiting for transfers between devices, per_device(): lax.psum_scatter(fc2_grad, 'dp', scatter_dimension=1, tiled=True)  120 us
    reduce_scatter x1, waiting for transfers between devices, per_device(): lax.psum_scatter(normed_back, 'tensor', scatter_dimension=0, tiled=True)  85 us
    all_gather x1, waiting for transfers between devices, per_device(): grad_all = lax.all_gather(out_grad, 'tensor', axis=0, tiled=True)  82.3 us
    all_gather x1, waiting for transfers between devices, per_device(): normed_all = lax.all_gather(normed, 'tensor', axis=0, tiled=True)  75.2 us
    all_gather x1, waiting for transfers between devices, per_device(): lax.all_gather(qkv_weight, 'dp', axis=1, tiled=True)  47.4 us
    psum x1, blocking collectives, per_device(): lax.psum((gain_part, shift_part, output_part), ('dp', 'tensor'))  41.3 us
  transfers between devices with their start and end apart: 12, of which 9 were waited for; matrix products, arithmetic and copies ran while one was open for 24% of the time, Pallas kernels for 0%

commit v1 on v0

--- a/solution.py
+++ b/solution.py
@@ -178,7 +178,30 @@
     summed = lax.psum_scatter(partial_value, "tensor", scatter_dimension=0, tiled=True)
     hidden_out = (inputs + summed + dense_bias + fc2_bias).astype(jnp.bfloat16)
     qkv_back, dense_back, fc1_back, fc2_back = (qkv_full, dense_full, fc1_full, fc2_full)
-    grad_all = lax.all_gather(out_grad, "tensor", axis=0, tiled=True)
+    local_part, value_now, all_rows = (
+        lax.psum(1, "tensor"),
+        lax.axis_index("tensor"),
+        out_grad.shape[0],
+    )
+    found = [hop_no * local_part if w == 0 else hop_no for w, hop_no in enumerate(out_grad.shape)]
+    grad_all = lax.dynamic_update_slice_in_dim(
+        jnp.zeros(found, out_grad.dtype), out_grad, value_now * all_rows, axis=0
+    )
+    n_now = tmp = out_grad
+    for k0 in tuple(range(1, local_part // 2 + 1)):
+        n_now = lax.ppermute(
+            n_now, "tensor", [(w, (w + 1) % local_part) for w in range(local_part)]
+        )
+        grad_all = lax.dynamic_update_slice_in_dim(
+            grad_all, n_now, (value_now - k0) % local_part * all_rows, axis=0
+        )
+        if 2 * k0 < local_part:
+            tmp = lax.ppermute(
+                tmp, "tensor", [(w, (w - 1) % local_part) for w in range(local_part)]
+            )
+            grad_all = lax.dynamic_update_slice_in_dim(
+                grad_all, tmp, (value_now + k0) % local_part * all_rows, axis=0
+            )
     feed_grad = dot_right(grad_all, fc2_back)
     unused, gelu_pull = jax.vjp(gelu_tanh, hidden)
     hidden_back = gelu_pull(feed_grad)[0].astype(jnp.bfloat16)

time: 1060 us -> 1020 us (0.962)
  waiting for transfers between devices: 708 us -> 649 us
    ppermute x0 -> x3, waiting for transfers between devices: none -> 95 us  [the longest x1 55.5 us: per_device(): lax.ppermute(tmp, 'tensor', [(w, (w - 1) % local_part) for w in range(loc...]
    all_gather x1 -> x0, waiting for transfers between devices: 82.3 us -> none  [per_device(): grad_all = lax.all_gather(out_grad, 'tensor', axis=0, tiled=True)]
    all_gather x1, waiting for transfers between devices: 75.2 us -> 24.9 us  [per_device(): normed_all = lax.all_gather(normed, 'tensor', axis=0, tiled=True)]
    all_gather x1, waiting for transfers between devices: 21.1 us -> 0.01 us  [per_device(): lax.all_gather(dense_weight, 'dp', axis=1, tiled=True)]
  transfers between devices with their start and end apart: 12 -> 14, of which waited for: 9 -> 10; matrix products, arithmetic and copies ran while one was open for 24% -> 26% of each run, Pallas kernels for 0% -> 0%
where the time goes in v1:
time: 1020 us; the launch traced here: 1010 us
  waiting for transfers between devices  649 us (64%)
  matrix products  200 us (20%)
  blocking collectives  65.6 us (6%)
  other arithmetic  43.8 us (4%)
  local copies, waits for them, and re-layouts  34.6 us (3%)
  between operations  14.9 us (1%)
    reduce_scatter x1, waiting for transfers between devices, per_device(): lax.psum_scatter(partial_value, 'tensor', scatter_dimension=0, tiled=True)  145 us
    reduce_scatter x1, waiting for transfers between devices, per_device(): lax.psum_scatter(fc1_grad, 'dp', scatter_dimension=0, tiled=True)  120 us
    reduce_scatter x1, waiting for transfers between devices, per_device(): lax.psum_scatter(fc2_grad, 'dp', scatter_dimension=1, tiled=True)  120 us
    reduce_scatter x1, waiting for transfers between devices, per_device(): lax.psum_scatter(normed_back, 'tensor', scatter_dimension=0, tiled=True)  84.8 us
    ppermute x1, waiting for transfers between devices, per_device(): lax.ppermute(tmp, 'tensor', [(w, (w - 1) % local_part) for w in range(loc...  55.5 us
    all_gather x1, waiting for transfers between devices, per_device(): lax.all_gather(qkv_weight, 'dp', axis=1, tiled=True)  48.2 us
    psum x1, blocking collectives, per_device(): lax.psum((gain_part, shift_part, output_part), ('dp', 'tensor'))  41.3 us
    dot_general x3, matrix products, dot_right(): lax.dot_general(left, right, (((1,), (1,)), ((), ())), preferred_element_...  40.7 us
  transfers between devices with their start and end apart: 14, of which 10 were waited for; matrix products, arithmetic and copies ran while one was open for 26% of the time, Pallas kernels for 0%

profile of v1, /device:TPU:0, one launch (start us, length us, event | category | flops | bytes accessed | tf_op | source)
XLA Modules:
  0.0 1014.0 jit_solution(15267071119040956395)
XLA Ops:
  11.7 2.7 fusion.30
  14.4 2.3 copy.24
  17.4 3.1 collective-permute-start
  20.5 2.1 collective-permute-start.1
  24.5 22.1 %collective-permute-done = bf16[256,2048]{1,0:T(8,128)(2,1)S(1)} collective-permute-done((bf16[256,2048]{1,0:T(8,128)(2,1)S(1)}, bf16[256,2048]{1,0:T(8,128)(2,1)S(1)}, u32[]{:S(2)}, u32[]{:S(2)}) %collective-permute-start) | collective-permute-done | bytes 1048608 | tf_op jit(solution)/shard_map/ppermute | solution.py:192
  47.7 2.6 broadcast_in_dim.24
  52.4 55.5 %collective-permute-done.1 = bf16[256,2048]{1,0:T(8,128)(2,1)S(1)} collective-permute-done((bf16[256,2048]{1,0:T(8,128)(2,1)S(1)}, bf16[256,2048]{1,0:T(8,128)(2,1)S(1)}, u32[]{:S(2)}, u32[]{:S(2)}) %collective-permute-start.1) | collective-permute-done | bytes 1048608 | tf_op jit(solution)/shard_map/ppermute | solution.py:199
  108.9 17.5 %collective-permute-done.2 = bf16[256,2048]{1,0:T(8,128)(2,1)S(1)} collective-permute-done((bf16[256,2048]{1,0:T(8,128)(2,1)S(1)}, bf16[256,2048]{1,0:T(8,128)(2,1)S(1)}, u32[]{:S(2)}, u32[]{:S(2)}) %collective-permute-start.2) | collective-permute-done | bytes 1048608 | tf_op jit(solution)/shard_map/ppermute | solution.py:192
  127.4 6.2 convolution_convert_fusion
  133.7 24.9 %all-gather.6.cloned.1.call-done = bf16[1024,2048]{1,0:T(8,128)(2,1)} async-done(((bf16[256,2048]{1,0:T(8,128)(2,1)}), bf16[1024,2048]{1,0:T(8,128)(2,1)}) %all-gather.6.cloned.1.call-update) | async-done | bytes 4194320 | tf_op jit(solution)/shard_map/all_gather | solution.py:155
  158.6 48.2 %all-gather.8.cloned.1.call-done = bf16[3,2048,512]{1,2,0:T(8,128)(2,1)} async-done(((bf16[3,256,512]{1,2,0:T(8,128)(2,1)}), bf16[3,2048,512]{1,2,0:T(8,128)(2,1)}) %all-gather.8.cloned.1.call-update) | async-done | bytes 6291472 | tf_op jit(solution)/shard_map/all_gather | solution.py:145
  206.8 10.6 %add_bitcast_fusion = f32[3,1024,512]{1,2,0:T(8,128)S(1)} fusion(f32[3,512]{1,0:T(4,128)S(1)} %copy-done.42, bf16[3,2048,512]{1,2,0:T(8,128)(2,1)} %all-gather.8.cloned.1.call-done, bf16[1024,2048]{1,0:T(8,128)(2,1)} %all-gather.6.cloned.1.call-done), kind=kOutput, calls=%fused_computation.33 | convolution fusion | flops 6444023808 | bytes 16783360 | tf_op jit(solution)/shard_map/td,cde->cte/dot_general | solution.py:165
  222.4 2.1 copy-done.1
  224.6 3.2 fusion.73
  227.9 3.8 fusion
  231.7 5.6 copy-done.2
  239.2 4.0 fusion.40
  243.2 2.3 copy.31
  245.5 7.6 multiply_reduce_fusion.1
  253.1 7.4 multiply_convert_fusion.1
  260.5 2.1 copy-done.3
  264.5 9.9 multiply_reduce_fusion
  274.3 10.3 %multiply_convert_fusion = bf16[8,512,1024]{2,1,0:T(8,128)(2,1)} fusion(f32[8,512,1024]{2,1,0:T(8,128)} %get-tuple-element.126, f32[8,512,1024]{2,1,0:T(8,128)S(1)} %bitcast.133, f32[8,512]{1,0:T(8,128)} %get-tuple-element.125, f32[8,512]{1,0:T(8,128)S(1)} %log_add_fusion), kind=kLoop, calls=%fused_computation | loop fusion | flops 16777216 | bytes 41975808 | tf_op jit(solution)/shard_map/convert_element_type | solution.py:103
  284.7 6.4 fusion.49
  297.7 2.3 copy.29
  300.0 2.3 copy.30
  302.3 12.4 %convolution_bitcast_fusion = f32[3,2048,512]{1,2,0:T(8,128)} fusion(bf16[1024,2048]{1,0:T(8,128)(2,1)} %all-gather.6.cloned.1.call-done, bf16[1,1024,512]{2,1,0:T(8,128)(2,1)S(1)} %copy-done.7, bf16[1,1024,512]{2,1,0:T(8,128)(2,1)} %copy.30, bf16[1,1024,512]{2,1,0:T(8,128)(2,1)} %copy.29), kind=kOutput, calls=%fused_computation.34 | convolution fusion | flops 6445596672 | bytes 19922944 | tf_op jit(solution)/shard_map/td,cte->cde/dot_general | solution.py:226
  314.8 14.7 %fusion.74 = f32[1024,2048]{1,0:T(8,128)} fusion(bf16[1024,2048]{1,0:T(8,128)(2,1)} %all-gather.6.cloned.1.call-done, bf16[2048,2048]{1,0:T(8,128)(2,1)} %all-gather.12.cloned.1.call-done), kind=kOutput, calls=%fused_computation.145 | convolution fusion | flops 8589934592 | bytes 20971520 | tf_op jit(solution)/shard_map/dot_general | solution.py:173
  329.4 23.0 %convert_reduce_fusion = (f32[2048]{0:T(1024)}, bf16[1024,2048]{1,0:T(8,128)(2,1)S(1)}) fusion(f32[1024,2048]{1,0:T(8,128)} %fusion.74, f32[2048]{0:T(1024)S(1)} %copy-done.43, bf16[1024,2048]{1,0:T(8,128)(2,1)} %constant_dynamic-update-slice_fusion, bf16[2048,2048]{1,0:T(8,128)(2,1)} %all-gather.14.cloned.1.call-done), kind=kOutput, calls=%fused_computation.20 | convolution fusion | flops 8646555648 | bytes 25182208 | tf_op jit(solution)/shard_map/dot_general | solution.py:13
  352.4 11.5 %fusion.75 = f32[1024,2048]{1,0:T(8,128)} fusion(bf16[1024,2048]{1,0:T(8,128)(2,1)S(1)} %get-tuple-element.98, bf16[2048,2048]{1,0:T(8,128)(2,1)S(1)} %copy-done.41), kind=kOutput, calls=%fused_computation.146 | convolution fusion | flops 8589934592 | bytes 20971520 | tf_op jit(solution)/shard_map/dot_general | solution.py:13
  364.0 13.1 %bitcast_add_fusion = f32[1024,2048]{1,0:T(8,128)} fusion(f32[1024,2048]{1,0:T(8,128)} %fusion.75, bf16[3,2048,512]{1,2,0:T(8,128)(2,1)} %all-gather.8.cloned.1.call-done, bf16[1,1024,512]{2,1,0:T(8,128)(2,1)S(1)} %copy-done.7, bf16[1,1024,512]{2,1,0:T(8,128)(2,1)S(1)} %copy-done.9, bf16[1,1024,512]{2,1,0:T(8,128)(2,1)S(1)} %copy-done.8), kind=kOutput, calls=%fused_computation.19 | convolution fusion | flops 6447693824 | bytes 26214400 | tf_op jit(solution)/shard_map/cte,cde->td/dot_general | solution.py:228
  377.8 5.0 fusion.53
  382.8 8.0 fusion.52
  391.0 12.2 %fusion.69 = f32[1024,2048]{1,0:T(8,128)S(1)} fusion(bf16[2048,2048]{1,0:T(8,128)(2,1)S(1)} %bitcast.159, f32[1024,2048]{1,0:T(8,128)} %fusion.74, f32[2048]{0:T(1024)S(1)} %copy-done.43), kind=kOutput, calls=%fused_computation.140 | convolution fusion | flops 8610906112 | bytes 25174016 | tf_op jit(solution)/shard_map/dot_general | solution.py:175
  403.2 5.7 convolution_add_fusion
  409.0 6.5 fusion.76
  415.5 17.4 %fusion.68 = f32[2048,2048]{1,0:T(8,128)} fusion(bf16[1024,2048]{1,0:T(8,128)(2,1)} %constant_dynamic-update-slice_fusion, f32[1024,2048]{1,0:T(8,128)} %fusion.74, f32[2048]{0:T(1024)S(1)} %copy-done.43), kind=kOutput, calls=%fused_computation.139 | convolution fusion | flops 8610906112 | bytes 29368320 | tf_op jit(solution)/shard_map/dot_general | solution.py:19
  433.1 15.4 %fusion.77 = f32[2048,2048]{1,0:T(8,128)} fusion(bf16[1024,2048]{1,0:T(8,128)(2,1)} %all-gather.6.cloned.1.call-done, bf16[1024,2048]{1,0:T(8,128)(2,1)} %copy-done.44), kind=kOutput, calls=%fused_computation.148 | convolution fusion | flops 8589934592 | bytes 25165824 | tf_op jit(solution)/shard_map/dot_general | solution.py:19
  450.6 24.3 %all-reduce.3 = (f32[3,512]{1,0:T(4,128)}, f32[2048]{0:T(1024)}) all-reduce(f32[3,512]{1,0:T(4,128)S(1)} %convert_reduce_fusion.1, f32[2048]{0:T(1024)S(1)} %copy-done.37), channel_id=1, replica_groups=mesh['dp'=8,'tensor'=4] {'dp'}, use_global_device_ids=true, to_apply=%region_14.15 | all-reduce | flops 3584 | bytes 28672 | tf_op jit(solution)/shard_map/psum | solution.py:244
  475.0 3.0 copy.34
  478.0 84.8 %reduce-scatter.9.cloned.1.call-done = f32[256,2048]{1,0:T(8,128)} async-done(((f32[1024,2048]{1,0:T(8,128)}), f32[256,2048]{1,0:T(8,128)}) %reduce-scatter.9.cloned.1.call-update) | async-done | bytes 2097168 | tf_op jit(solution)/shard_map/reduce_scatter | solution.py:231
  562.8 2.6 fusion.34
  565.4 145.0 %reduce-scatter.7.cloned.1.call-done = f32[256,2048]{1,0:T(8,128)} async-done(((f32[1024,2048]{1,0:T(8,128)}), f32[256,2048]{1,0:T(8,128)}) %reduce-scatter.7.cloned.1.call-update) | async-done | bytes 2097168 | tf_op jit(solution)/shard_map/reduce_scatter | solution.py:178
  710.4 5.1 convert_reduce_fusion.3
  715.5 41.3 %all-reduce.2 = (f32[2048]{0:T(1024)S(1)}, f32[2048]{0:T(1024)}, f32[2048]{0:T(1024)}) all-reduce(f32[2048]{0:T(1024)S(1)} %get-tuple-element.109, f32[2048]{0:T(1024)S(1)} %get-tuple-element.88, f32[2048]{0:T(1024)S(1)} %get-tuple-element.91), channel_id=1, replica_groups=mesh['dp'=8,'tensor'=4] {'dp','tensor'}, use_global_device_ids=true, to_apply=%region_17.18 | all-reduce | flops 6144 | bytes 49152 | tf_op jit(solution)/shard_map/psum | solution.py:241
  756.9 9.4 reduce-scatter.13.cloned.1.call-done
  766.3 120.0 %reduce-scatter.17.cloned.1.call-done = f32[2048,256]{1,0:T(8,128)} async-done(((f32[2048,2048]{1,0:T(8,128)}), f32[2048,256]{1,0:T(8,128)}) %reduce-scatter.17.cloned.1.call-update) | async-done | bytes 2097168 | tf_op jit(solution)/shard_map/reduce_scatter | solution.py:249
  886.3 120.4 %reduce-scatter.15.cloned.1.call-done = f32[256,2048]{1,0:T(8,128)} async-done(((f32[2048,2048]{1,0:T(8,128)}), f32[256,2048]{1,0:T(8,128)}) %reduce-scatter.15.cloned.1.call-update) | async-done | bytes 2097168 | tf_op jit(solution)/shard_map/reduce_scatter | solution.py:248
  (172 shorter events, 31.6 us)
Async XLA Ops:
  7.2 10.2 %copy-start.11 = (bf16[256,2048]{1,0:T(8,128)(2,1)S(1)}, bf16[256,2048]{1,0:T(8,128)(2,1)}, u32[]{:S(2)}) copy-start(bf16[256,2048]{1,0:T(8,128)(2,1)} %param.35) | copy-start | bytes 3145732
  7.2 120.2 %all-gather.10.cloned.1.call-start = ((), (), s32[]{:S(2)}) async-start(), calls=%async_computation.8 | async-start | bytes 2359296 | tf_op jit(solution)/shard_map/all_gather | solution.py:146
  7.9 150.6 %all-gather.6.cloned.1.call-start = ((), (), s32[]{:S(2)}) async-start(), calls=%async_computation.6 | async-start | bytes 5242880 | tf_op jit(solution)/shard_map/all_gather | solution.py:155
  14.4 192.4 %all-gather.8.cloned.1.call-start = ((), (), s32[]{:S(2)}) async-start(), calls=%async_computation.7 | async-start | bytes 7077888 | tf_op jit(solution)/shard_map/all_gather | solution.py:145
  16.7 298.0 %all-gather.12.cloned.1.call-start = ((), (), s32[]{:S(2)}) async-start(), calls=%async_computation.9 | async-start | bytes 9437184 | tf_op jit(solution)/shard_map/all_gather | solution.py:147
  17.3 312.1 %all-gather.14.cloned.1.call-start = ((), (), s32[]{:S(2)}) async-start(), calls=%async_computation.10 | async-start | bytes 9437184 | tf_op jit(solution)/shard_map/all_gather | solution.py:148
  17.4 29.2 %collective-permute-start = (bf16[256,2048]{1,0:T(8,128)(2,1)S(1)}, bf16[256,2048]{1,0:T(8,128)(2,1)S(1)}, u32[]{:S(2)}, u32[]{:S(2)}) collective-permute-start(bf16[256,2048]{1,0:T(8,128)(2,1)S(1)} %copy-done.11), channel_id=1, source_target_pairs={{0,1},{1,2},{2,3},{3,0},{4,5},{5,6},{6,7},{7,4},{8,9},{9,10},{10,1... | collective-permute-start | bytes 3145736 | tf_op jit(solution)/shard_map/ppermute | solution.py:192
  20.5 87.4 %collective-permute-start.1 = (bf16[256,2048]{1,0:T(8,128)(2,1)S(1)}, bf16[256,2048]{1,0:T(8,128)(2,1)S(1)}, u32[]{:S(2)}, u32[]{:S(2)}) collective-permute-start(bf16[256,2048]{1,0:T(8,128)(2,1)S(1)} %copy-done.11), channel_id=1, source_target_pairs={{0,3},{1,0},{2,1},{3,2},{4,7},{5,4},{6,5},{7,6},{8,11},{9,8},{10,9... | collective-permute-start | bytes 3145736 | tf_op jit(solution)/shard_map/ppermute | solution.py:199
  22.6 452.4 %reduce-scatter.11.cloned.1.call-start = ((), (), s32[]{:S(2)}) async-start(), calls=%async_computation.13 | async-start | bytes 14155776 | tf_op jit(solution)/shard_map/reduce_scatter | solution.py:246
  46.5 79.8 %collective-permute-start.2 = (bf16[256,2048]{1,0:T(8,128)(2,1)S(1)}, bf16[256,2048]{1,0:T(8,128)(2,1)S(1)}, u32[]{:S(2)}, u32[]{:S(2)}) collective-permute-start(bf16[256,2048]{1,0:T(8,128)(2,1)S(1)} %collective-permute-done), channel_id=1, source_target_pairs={{0,1},{1,2},{2,3},{3,0},{4,5},{5,6},{6,7},{7,4},{8,9},{9,10},{10,1... | collective-permute-start | bytes 3145736 | tf_op jit(solution)/shard_map/ppermute | solution.py:192
  127.4 79.4 %copy-start.42 = (f32[3,512]{1,0:T(4,128)S(1)}, f32[3,512]{1,0:T(4,128)}, u32[]{:S(2)}) copy-start(f32[3,512]{1,0:T(4,128)} %param.26) | copy-start | bytes 18436
  218.2 6.4 copy-start.14
  221.2 6.6 copy-start.25
  224.6 20.9 %copy-start.23 = (f32[8,512]{1,0:T(8,128)}, f32[8,512]{1,0:T(8,128)S(1)}, u32[]{:S(2)}) copy-start(f32[8,512]{1,0:T(8,128)S(1)} %log_add_fusion.1) | copy-start | bytes 49156
  227.8 11.4 %copy-start = (f32[8,512,1024]{2,1,0:T(8,128)}, f32[8,512,1024]{2,1,0:T(8,128)S(1)}, u32[]{:S(2)}) copy-start(f32[8,512,1024]{2,1,0:T(8,128)S(1)} %get-tuple-element.122) | copy-start | bytes 50331652
  227.8 9.4 copy-start.2
  227.8 10.0 copy-start.6
  231.6 11.6 %copy-start.31 = (f32[8,512]{1,0:T(8,128)}, f32[8,512]{1,0:T(8,128)S(1)}, u32[]{:S(2)}) copy-start(f32[8,512]{1,0:T(8,128)S(1)} %fusion) | copy-start | bytes 49156
  245.5 19.0 %slice-start = ((s8[16777216]{0:T(1024)(128)(4,1)}), s8[4194304]{0:T(1024)(128)(4,1)S(1)}, s32[]{:S(2)}) async-start(s8[16777216]{0:T(1024)(128)(4,1)} %bitcast.132), calls=%async_computation.17 | async-start | bytes 8388608
  245.5 19.0 %slice-start.1 = ((s8[16777216]{0:T(1024)(128)(4,1)}), s8[4194304]{0:T(1024)(128)(4,1)S(1)}, s32[]{:S(2)}) async-start(s8[16777216]{0:T(1024)(128)(4,1)} %bitcast.132), calls=%async_computation.18 | async-start | bytes 8388608
  253.1 9.6 copy-start.16
  253.1 11.4 %slice-start.2 = ((s8[16777216]{0:T(1024)(128)(4,1)}), s8[4194304]{0:T(1024)(128)(4,1)S(1)}, s32[]{:S(2)}) async-start(s8[16777216]{0:T(1024)(128)(4,1)} %bitcast.132), calls=%async_computation.19 | async-start | bytes 8388608
  253.1 11.4 %slice-start.3 = ((s8[16777216]{0:T(1024)(128)(4,1)}), s8[4194304]{0:T(1024)(128)(4,1)S(1)}, s32[]{:S(2)}) async-start(s8[16777216]{0:T(1024)(128)(4,1)} %bitcast.132), calls=%async_computation.20 | async-start | bytes 8388608
  284.7 6.4 copy-start.10
  284.7 6.6 copy-start.4
  284.7 8.0 slice-start.4
  295.8 6.5 copy-start.7
  314.7 14.8 %copy-start.43 = (f32[2048]{0:T(1024)S(1)}, f32[2048]{0:T(1024)}, u32[]{:S(2)}) copy-start(f32[2048]{0:T(1024)} %param.30) | copy-start | bytes 24580
  314.7 248.1 %reduce-scatter.9.cloned.1.call-start = ((), (), s32[]{:S(2)}) async-start(), calls=%async_computation.12 | async-start | bytes 10485760 | tf_op jit(solution)/shard_map/reduce_scatter | solution.py:231
  329.4 23.0 %copy-start.41 = (bf16[2048,2048]{1,0:T(8,128)(2,1)S(1)}, bf16[2048,2048]{1,0:T(8,128)(2,1)}, u32[]{:S(2)}) copy-start(bf16[2048,2048]{1,0:T(8,128)(2,1)} %all-gather.12.cloned.1.call-done) | copy-start | bytes 25165828
  352.4 11.6 %copy-start.44 = (bf16[1024,2048]{1,0:T(8,128)(2,1)}, bf16[1024,2048]{1,0:T(8,128)(2,1)S(1)}, u32[]{:S(2)}) copy-start(bf16[1024,2048]{1,0:T(8,128)(2,1)S(1)} %get-tuple-element.98) | copy-start | bytes 12582916
  352.4 11.6 %copy-start.8 = (bf16[1,1024,512]{2,1,0:T(8,128)(2,1)S(1)}, bf16[1,1024,512]{2,1,0:T(8,128)(2,1)}, u32[]{:S(2)}) copy-start(bf16[1,1024,512]{2,1,0:T(8,128)(2,1)} %copy.29) | copy-start | bytes 3145732
  352.4 11.6 %copy-start.9 = (bf16[1,1024,512]{2,1,0:T(8,128)(2,1)S(1)}, bf16[1,1024,512]{2,1,0:T(8,128)(2,1)}, u32[]{:S(2)}) copy-start(bf16[1,1024,512]{2,1,0:T(8,128)(2,1)} %copy.30) | copy-start | bytes 3145732
  377.1 333.3 %reduce-scatter.7.cloned.1.call-start = ((), (), s32[]{:S(2)}) async-start(), calls=%async_computation.11 | async-start | bytes 10485760 | tf_op jit(solution)/shard_map/reduce_scatter | solution.py:178
  377.8 13.2 %slice-start.6 = ((s8[8388608]{0:T(1024)(128)(4,1)}), s8[4194304]{0:T(1024)(128)(4,1)S(1)}, s32[]{:S(2)}) async-start(s8[8388608]{0:T(1024)(128)(4,1)} %bitcast.158), calls=%async_computation.23 | async-start | bytes 8388608
  382.8 8.1 slice-start.7
  391.0 12.2 %copy-start.13 = (bf16[512,2048]{1,0:T(8,128)(2,1)S(1)}, bf16[512,2048]{1,0:T(8,128)(2,1)}, u32[]{:S(2)}) copy-start(bf16[512,2048]{1,0:T(8,128)(2,1)} %all-gather.10.cloned.1.call-done) | copy-start | bytes 6291460
  408.9 357.4 %reduce-scatter.13.cloned.1.call-start = ((), (), s32[]{:S(2)}) async-start(), calls=%async_computation.14 | async-start | bytes 4718592 | tf_op jit(solution)/shard_map/reduce_scatter | solution.py:247
  415.5 470.8 %reduce-scatter.17.cloned.1.call-start = ((), (), s32[]{:S(2)}) async-start(), calls=%async_computation.16 | async-start | bytes 18874368 | tf_op jit(solution)/shard_map/reduce_scatter | solution.py:249
  433.0 573.6 %reduce-scatter.15.cloned.1.call-start = ((), (), s32[]{:S(2)}) async-start(), calls=%async_computation.15 | async-start | bytes 18874368 | tf_op jit(solution)/shard_map/reduce_scatter | solution.py:248
  448.5 114.3 %copy-start.5 = (bf16[256,2048]{1,0:T(8,128)(2,1)S(1)}, bf16[256,2048]{1,0:T(8,128)(2,1)}, u32[]{:S(2)}) copy-start(bf16[256,2048]{1,0:T(8,128)(2,1)} %param.24) | copy-start | bytes 3145732
  448.5 114.3 %copy-start.24 = (f32[2048]{0:T(1024)S(1)}, f32[2048]{0:T(1024)}, u32[]{:S(2)}) copy-start(f32[2048]{0:T(1024)} %param.33) | copy-start | bytes 24580
  448.5 114.3 %copy-start.34 = (f32[256]{0:T(256)S(1)}, f32[256]{0:T(256)}, u32[]{:S(2)}) copy-start(f32[256]{0:T(256)} %copy-done.33) | copy-start | bytes 3076
  448.5 114.3 %copy-start.36 = (f32[256]{0:T(256)S(1)}, f32[256]{0:T(256)}, u32[]{:S(2)}) copy-start(f32[256]{0:T(256)} %copy-done.35) | copy-start | bytes 3076
  448.5 261.9 %copy-start.39 = (f32[2048]{0:T(1024)S(1)}, f32[2048]{0:T(1024)}, u32[]{:S(2)}) copy-start(f32[2048]{0:T(1024)} %param.32) | copy-start | bytes 24580
  448.5 261.9 %copy-start.40 = (f32[2048]{0:T(1024)S(1)}, f32[2048]{0:T(1024)}, u32[]{:S(2)}) copy-start(f32[2048]{0:T(1024)} %param.28) | copy-start | bytes 24580
  450.6 259.8 %copy-start.12 = (bf16[256,2048]{1,0:T(8,128)(2,1)S(1)}, bf16[256,2048]{1,0:T(8,128)(2,1)}, u32[]{:S(2)}) copy-start(bf16[256,2048]{1,0:T(8,128)(2,1)} %param.35) | copy-start | bytes 3145732
  756.8 250.4 %copy-start.38 = (f32[2048]{0:T(1024)}, f32[2048]{0:T(1024)S(1)}, u32[]{:S(2)}) copy-start(f32[2048]{0:T(1024)S(1)} %get-tuple-element.150) | copy-start | bytes 24580
  (19 other events, 44.0 us)
Sparse Core Ops, SparseCore 0:
  9.9 30.8 all-gather.9
  42.9 115.6 all-gather.5
  161.0 45.7 all-gather.7
  208.5 54.2 all-gather.11
  264.5 55.8 all-gather.13
  323.8 91.9 reduce-scatter.10
  418.1 144.6 reduce-scatter.8
  565.1 145.2 reduce-scatter.6
  714.4 51.8 reduce-scatter.12
  770.2 115.9 reduce-scatter.16
  890.4 116.1 reduce-scatter.14
